TPU v7x, 32 devices: a whole 2x2x4 slice. The times are simulated.
32 devices in a mesh: groups: 2 (over x), blk: 16 (over z, y, core).
Axes of the slice: x: 2, y: 2, z: 4, core: 2. Of those that a mesh axis runs over, the one named last changes fastest.
Arguments:
- tokens: bfloat16 [2048, 4096], P(('groups', 'blk')), parts along dimension 0, may hold values from -9 to 9, as said below
- blocks: bfloat16 [16, 7, 128, 128], P('blk'), may hold values from -0.5 to 0.5
- counts: int32 [2, 8], replicated, may hold values from 1 to 7, 48 in all within a row
- block_rows: int32 [16, 7], replicated, may hold values from 0 to 31
- block_cols: int32 [16, 7], replicated, may hold values from 0 to 111
Outputs:
- up: bfloat16 [2048, 14336], P(('groups', 'blk')), parts along dimension 0
- col_rms: float32 [28672], P('groups'), parts along dimension 0
There are 2 independent parts, one for each index of `groups`. A program takes and returns all parts, laid end to end along the dimension named above; an argument that names none is the same for every part. Nothing has to cross between parts.
Inputs may be any that keep to these rules, and one draw needn't show every extreme that they name: `tokens`: scale of a token's entries grows with its position in the sequence. `counts`: each row sums to 48, and each row has an entry equal to 7. `block_rows`: slots at or past an owner's count carry no block and are ignored, whatever they hold. `block_cols`: slots at or past an owner's count are ignored.
All inputs are finite; a program needn't handle non-finite values.
Results may differ from a plain program's by a relative error of at most 0.001.
Values may be sent and summed in bfloat16 or wider, within the bound.
A program may use at most 192 MiB of HBM per device.

v0:
```python
import functools

import jax
import jax.numpy as jnp
from jax import lax
from jax.experimental import pallas as pl
from jax.experimental.pallas import tpu as pltpu
from jax.sharding import PartitionSpec as P

FFW = 14336
MESH = pl.DeviceIdType.MESH
VMEM_ROOM = 67043328


def ring_place(chip, chips):
    odd, half = chip % 2, chip // 2
    return (1 - odd) * half + odd * (chips - 1 - half)


def chip_at(place, chips):
    high = place // (chips // 2)
    return (1 - high) * 2 * place + high * (2 * (chips - 1 - place) + 1)


def kernel(
    n, slots, ring_slots, cols,
    counts_ref, rows_ref, cols_ref, cols_v, tok_hbm, blocks_hbm, up_hbm, rms_ref,
    tok_ref, blocks_ref, prev_v, last_v, prev_ref, last_ref, held, tok_s, up_ref, sums, sq_s, red_s, res_s,
    ring_send, ring_recv, x_send, x_recv, pd_send, pd_recv,
    own_send, own_recv, end_send, end_recv, a_send, a_recv, b_send, b_recv, in_sem, up_sem,
):
    chips = n // 2
    half = chips // 2
    edge = blocks_ref.shape[-1]
    via_x = slots - ring_slots
    me, g = lax.axis_index("blk"), lax.axis_index("groups")
    chip, core = me // 2, me % 2
    place = ring_place(chip, chips)
    partner = chip * 2 + 1 - core
    towards = [
        chip_at((place + 1) % chips, chips) * 2 + core,
        chip_at((place + chips - 1) % chips, chips) * 2 + core,
    ]

    def owner(step, way, mine=True):
        at = (place - step + chips) % chips if way == 0 else (place + step) % chips
        return chip_at(at, chips) * 2 + (core if mine else 1 - core)

    def near(i):
        return g * (slots - 1) + i * (1 - 2 * g)

    def far(i):
        return (1 - g) * (slots - 1) + i * (2 * g - 1)

    def slot_of(i):
        return near(i) if i < ring_slots else far(i - ring_slots)

    def last_list(way):
        return [i for i in range(slots) if i % 2 == way]

    blocks_in = pltpu.make_async_copy(blocks_hbm, blocks_ref, in_sem.at[0])
    tok_in = pltpu.make_async_copy(tok_hbm, tok_ref, in_sem.at[1])
    blocks_in.start()
    tok_in.start()
    barrier = pltpu.get_barrier_semaphore()
    for to in ((g, towards[0]), (g, towards[1]), (g, partner), (1 - g, me)):
        pl.semaphore_signal(barrier, inc=1, device_id=to, device_id_type=MESH)
    sums[n * slots] = jnp.zeros(sums.shape[1:], sums.dtype)
    blocks_in.wait()
    pl.semaphore_wait(barrier, 4)

    sent = []

    def ring(step, way, i, start):
        o = owner(step - 1, way) if start else owner(step, way)
        s = slot_of(i)
        src = blocks_ref.at[0, s] if start and step == 1 else held.at[o, s]
        return pltpu.make_async_remote_copy(
            src_ref=src,
            dst_ref=held.at[o, s],
            send_sem=ring_send.at[way, step - 1, i],
            recv_sem=ring_recv.at[way, step - 1, i],
            device_id=(g, towards[way]),
            device_id_type=MESH,
        )

    def cross(step, way, i, start):
        o = owner(step, way)
        s = near(i) if start else far(i)
        return pltpu.make_async_remote_copy(
            src_ref=held.at[o, s],
            dst_ref=held.at[o, s],
            send_sem=x_send.at[way, step - 1, i],
            recv_sem=x_recv.at[way, step - 1, i],
            device_id=(1 - g, me),
            device_id_type=MESH,
        )

    def pair(step, way, start):
        o = owner(step, way, start)
        return pltpu.make_async_remote_copy(
            src_ref=held.at[o],
            dst_ref=held.at[o],
            send_sem=pd_send.at[way, step - 1],
            recv_sem=pd_recv.at[way, step - 1],
            device_id=(g, partner),
            device_id_type=MESH,
        )

    def pair_end(i, start):
        o = owner(half, 0, start)
        s = slot_of(i)
        return pltpu.make_async_remote_copy(
            src_ref=held.at[o, s],
            dst_ref=held.at[o, s],
            send_sem=end_send.at[i],
            recv_sem=end_recv.at[i],
            device_id=(g, partner),
            device_id_type=MESH,
        )

    def pair_own(start):
        o = me if start else partner
        return pltpu.make_async_remote_copy(
            src_ref=blocks_ref.at[0],
            dst_ref=held.at[o],
            send_sem=own_send,
            recv_sem=own_recv,
            device_id=(g, partner),
            device_id_type=MESH,
        )

    def go(copy):
        copy.start()
        sent.append(copy)

    for i in range(ring_slots):
        for way in (0, 1):
            go(ring(1, way, i, True))
    go(pair_own(True))

    def position(o):
        apart = (ring_place(o // 2, chips) - place + chips) % chips
        step = jnp.minimum(apart, chips - apart)
        rank = jnp.where(apart < half, 2 * step, 2 * step - 1)
        rank = jnp.where(apart == half, chips - 1, rank)
        rank = jnp.where(apart == 0, 0, rank)
        return rank * 2 + jnp.where(o % 2 == core, 0, 1)

    spare = n * slots
    shape = (slots, n)
    keys = position(lax.broadcasted_iota(jnp.int32, shape, 1)) * slots
    keys = keys + lax.broadcasted_iota(jnp.int32, shape, 0)
    at_col = lax.broadcasted_iota(jnp.int32, (1, cols), 1)
    here = cols_v[...]
    prev = jnp.full(shape, -1, jnp.int32)
    last = jnp.full((1, cols), -1, jnp.int32)
    per_row = counts_ref.shape[1]
    for o in range(n):
        base = position(jnp.int32(o)) * slots
        alive = counts_ref[o // per_row, o % per_row]
        for j in range(slots):
            key = jnp.where(alive > j, base + j, -1)
            col = cols_ref[j, o]
            prev = jnp.where((here == col) & (keys > key), jnp.maximum(prev, key), prev)
            last = jnp.where(at_col == col, jnp.maximum(last, key), last)
    prev_v[...] = jnp.where(prev < 0, spare, prev)
    last_v[...] = jnp.where(last < 0, spare, last)
    tok_in.wait()
    for r in range(tok_s.shape[0]):
        tok_s[r] = tok_ref[:, r * edge : (r + 1) * edge]
    prev_in = pltpu.make_async_copy(prev_v, prev_ref, in_sem.at[2])
    last_in = pltpu.make_async_copy(last_v, last_ref, in_sem.at[3])
    prev_in.start()
    last_in.start()
    prev_in.wait()
    last_in.wait()

    def terms(o, weights, pos):
        found = []
        alive = counts_ref[o // per_row, o % per_row]
        for j in range(slots):
            found.append(
                jnp.dot(
                    tok_s[jnp.where(alive > j, rows_ref[j, o], 0)],
                    weights[j],
                    preferred_element_type=jnp.float32,
                )
            )
        for j in range(slots):
            sums[pos * slots + j] = found[j] + sums[prev_ref[j, o]]

    terms(me, blocks_ref.at[0], 0)
    pending = []

    def partner_own():
        pair_own(False).wait_recv()
        terms(partner, held.at[partner], 1)

    pending.append(partner_own)

    def ring_task(step, way, rank, mine):
        o = owner(step, way, mine)
        if not mine:
            pair(step, way, False).wait_recv()
        terms(o, held.at[o], rank * 2 + (0 if mine else 1))

    def settle(step):
        for way in (0, 1):
            for i in range(via_x):
                cross(step, way, i, False).wait_recv()
                if step + 1 == half and (ring_slots + i) in last_list(way):
                    go(ring(half, way, ring_slots + i, True))
        for way in (0, 1):
            go(pair(step, way, True))
            for mine in (True, False):
                pending.append(
                    functools.partial(ring_task, step, way, 2 * step - 1 + way, mine)
                )

    def pop():
        if pending:
            pending.pop(0)()

    for step in range(1, half):
        for i in range(ring_slots):
            for way in (0, 1):
                ring(step, way, i, False).wait_recv()
                if step + 1 < half or i in last_list(way):
                    go(ring(step + 1, way, i, True))
                if i < via_x:
                    go(cross(step, way, i, True))
            if step > 1 and i == 1:
                settle(step - 1)
            pop()
    settle(half - 1)
    pop()
    pop()
    for i in range(slots):
        ring(half, i % 2, i, False).wait_recv()
        go(pair_end(i, True))
        if i % 2 == 0 and i < slots - 1:
            pop()
    while pending:
        pop()
    ring_task(half, 0, chips - 1, True)
    for i in range(slots):
        pair_end(i, False).wait_recv()
    terms(owner(half, 0, False), held.at[owner(half, 0, False)], n - 1)

    share = cols // n
    scatter, spread, up_out = {}, [], []
    wide = share * edge
    order = sorted(range(1, n), key=lambda e: abs(e - n // 2)) + [0]
    for at, e in enumerate(order):
        o = (me + e) % n
        found = []
        for j in range(share):
            c = o * share + j
            value = sums[last_ref[0, c]]
            up_ref[:, pl.ds(pl.multiple_of(c * edge, edge), edge)] = value.astype(up_ref.dtype)
            found.append(jnp.sum(value * value, axis=0, keepdims=True))
        sq_s[o] = jnp.concatenate(found, axis=0)
        if at > 0:
            before = order[at - 1]
            to = (me + before) % n
            scatter[before] = pltpu.make_async_remote_copy(
                src_ref=sq_s.at[to],
                dst_ref=red_s.at[before],
                send_sem=a_send.at[before],
                recv_sem=a_recv.at[before],
                device_id=(g, to),
                device_id_type=MESH,
            )
            scatter[before].start()
        span = pl.ds(pl.multiple_of(o * wide, wide), wide)
        up_out.append(
            pltpu.make_async_copy(up_ref.at[:, span], up_hbm.at[:, span], up_sem.at[e])
        )
        if at > 0:
            up_out[at - 1].start()
    up_out[-1].start()
    total = sq_s[me]
    for e in range(1, n):
        scatter[e].wait_recv()
        total = total + red_s[e]
    res_s[me] = jnp.sqrt(total / (tok_ref.shape[0] * n) + 1e-06)
    for e in range(1, n):
        to = (me + e) % n
        spread.append(
            pltpu.make_async_remote_copy(
                src_ref=res_s.at[me],
                dst_ref=res_s.at[me],
                send_sem=b_send.at[e],
                recv_sem=b_recv.at[e],
                device_id=(g, to),
                device_id_type=MESH,
            )
        )
        spread[-1].start()
    for copy in sent + list(scatter.values()):
        copy.wait_send()
    for e in range(1, n):
        origin = (me + n - e) % n
        pltpu.make_async_remote_copy(
            src_ref=res_s.at[origin],
            dst_ref=res_s.at[origin],
            send_sem=b_send.at[e],
            recv_sem=b_recv.at[e],
            device_id=(g, origin),
            device_id_type=MESH,
        ).wait_recv()
    for copy in spread:
        copy.wait_send()
    for copy in up_out:
        copy.wait()
    for o in range(n):
        rms_ref[o * share : (o + 1) * share, :] = res_s[o]


def per_device(n, tokens, blocks, counts, block_rows, block_cols):
    toks, width = tokens.shape
    _, slots, edge, _ = blocks.shape
    cols = FFW // edge
    share = cols // n
    half = n // 4
    ring_slots = slots - slots * 2 // 7
    via_x = slots - ring_slots
    rows, places = block_rows.T, block_cols.T
    hbm = pl.BlockSpec(memory_space=pltpu.HBM)
    vmem = pl.BlockSpec(memory_space=pltpu.VMEM)
    smem = pl.BlockSpec(memory_space=pltpu.SMEM)
    dma = pltpu.SemaphoreType.DMA
    up, rms = pl.pallas_call(
        functools.partial(kernel, n, slots, ring_slots, cols),
        out_shape=(
            jax.ShapeDtypeStruct((toks, FFW), jnp.bfloat16),
            jax.ShapeDtypeStruct((cols, edge), jnp.float32),
        ),
        in_specs=[smem, smem, smem, vmem, hbm, hbm],
        out_specs=(hbm, vmem),
        scratch_shapes=[
            pltpu.VMEM(tokens.shape, jnp.bfloat16),
            pltpu.VMEM(blocks.shape, jnp.bfloat16),
            pltpu.VMEM(places.shape, jnp.int32),
            pltpu.VMEM((1, cols), jnp.int32),
            pltpu.SMEM(places.shape, jnp.int32),
            pltpu.SMEM((1, cols), jnp.int32),
            pltpu.VMEM((n, slots, edge, edge), jnp.bfloat16),
            pltpu.VMEM((width // edge, toks, edge), jnp.bfloat16),
            pltpu.VMEM((toks, FFW), jnp.bfloat16),
            pltpu.VMEM((n * slots + 1, toks, edge), jnp.float32),
            pltpu.VMEM((n, share, edge), jnp.float32),
            pltpu.VMEM((n, share, edge), jnp.float32),
            pltpu.VMEM((n, share, edge), jnp.float32),
            dma((2, half, slots)),
            dma((2, half, slots)),
            dma((2, half, via_x)),
            dma((2, half, via_x)),
            dma((2, half)),
            dma((2, half)),
            dma,
            dma,
            dma((slots,)),
            dma((slots,)),
            dma((n,)),
            dma((n,)),
            dma((n,)),
            dma((n,)),
            dma((4,)),
            dma((n,)),
        ],
        compiler_params=pltpu.CompilerParams(
            collective_id=0, has_side_effects=True, vmem_limit_bytes=VMEM_ROOM
        ),
    )(counts, rows, places, places, tokens, blocks)
    return up, rms.reshape(-1)


def make_fold(token_grid, rows_table, cols_table, live_table, col_blocks):
    row_blocks = token_grid.shape[1]

    def fold(carry, piece, start):
        rows = rows_table.reshape(-1)
        cols = cols_table.reshape(-1)
        live = live_table.reshape(-1)
        weights = piece.reshape(-1, piece.shape[2], piece.shape[3])
        weights = jnp.where(live[:, None, None], weights, jnp.zeros_like(weights))
        row_pick = (rows[:, None] == jnp.arange(row_blocks, dtype=jnp.int32)[None, :]).astype(
            jnp.bfloat16
        )
        chosen = jnp.einsum(
            "trk,br->tbk", token_grid, row_pick, preferred_element_type=jnp.float32
        ).astype(jnp.bfloat16)
        terms = jnp.einsum("tbk,bkn->tbn", chosen, weights, preferred_element_type=jnp.float32)
        col_pick = (cols[:, None] == jnp.arange(col_blocks, dtype=jnp.int32)[None, :]).astype(
            jnp.float32
        )
        placed = jnp.einsum(
            "tbn,bc->tcn",
            terms,
            col_pick,
            precision=lax.Precision.HIGHEST,
            preferred_element_type=jnp.float32,
        )
        return placed.reshape(carry.shape)

    return fold


def by_collectives(tokens, blocks, counts, block_rows, block_cols):
    tok_count = tokens.shape[0]
    edge = blocks.shape[2]
    slots = blocks.shape[1]
    token_grid = tokens.reshape(tok_count, -1, edge)
    col_blocks = FFW // edge
    empty = jnp.zeros((tok_count, FFW), jnp.float32)
    live_table = counts.reshape(-1)[:, None] > jnp.arange(slots, dtype=jnp.int32)[None, :]
    fold = make_fold(token_grid, block_rows, block_cols, live_table, col_blocks)
    product = fold(empty, lax.all_gather(blocks, "blk", axis=0, tiled=True), jnp.int32(0))
    up = product.astype(jnp.bfloat16)
    squares = lax.psum(jnp.sum(product * product, axis=0), "blk")
    col_rms = jnp.sqrt(squares / (tok_count * lax.axis_size("blk")) + 1e-06)
    return (up, col_rms)


def solution(mesh):
    n, groups = mesh.shape["blk"], mesh.shape["groups"]

    def body(tokens, blocks, counts, block_rows, block_cols):
        owned, slots, edge, _ = blocks.shape
        cols = FFW // edge
        need = n * slots * edge * (2 * edge + 4 * tokens.shape[0])
        fits = need + 2 * tokens.shape[0] * (FFW + tokens.shape[1]) < VMEM_ROOM // 2
        if groups == 2 and owned == 1 and n % 4 == 0 and n >= 8 and cols % n == 0 and fits:
            return per_device(n, tokens, blocks, counts, block_rows, block_cols)
        return by_collectives(tokens, blocks, counts, block_rows, block_cols)

    placed = (P(("groups", "blk"), None), P("blk", None, None, None), P(), P(), P())
    return jax.shard_map(
        body,
        mesh=mesh,
        in_specs=placed,
        out_specs=(P(("groups", "blk"), None), P("groups")),
        check_vma=False,
    )
```

profile of v0, /device:TPU:0, one launch (start us, length us, event | category | flops | bytes accessed | tf_op | source)
XLA Modules:
  0.0 39.0 jit_solution(17936997248274446734)
XLA Ops:
  0.6 34.9 %shard_map.68 = (bf16[64,14336]{1,0:T(8,128)(2,1)}, f32[112,128]{1,0:T(8,128)}) custom-call(s32[2,8]{1,0:T(2,128)} %counts_ref.1, s32[7,16]{1,0:T(8,128)} %bitcast.6, s32[7,16]{1,0:T(8,128)} %bitcast.4, s32[7,16]{1,0:T(8,128)} %bitcast.5, bf16[64,4096]{1,0:T(8,128)(2,1)} %tok_hbm.1, bf16[1,7,128,128]{3,2,1,0:T(8,128)(2,1)} %blocks_hbm.1), custom_call_target="tpu_custom_call" | custom-call | tf_op jit(solution)/shard_map/pallas_call | solution.py:334
  35.5 0.0 copy-start
  35.5 2.9 %copy.9 = bf16[64,14336]{1,0:T(8,128)(2,1)} copy(bf16[64,14336]{1,0:T(8,128)(2,1)} %get-tuple-element.8) | data formatting | bytes 3670016
  38.4 0.0 copy-done
  38.4 0.6 %copy.10 = f32[14336]{0:T(1024)} copy(f32[14336]{0:T(1024)S(1)} %bitcast.3) | data formatting | bytes 114688
Async XLA Ops:
  35.5 2.9 %copy-start = (f32[112,128]{1,0:T(8,128)S(1)}, f32[112,128]{1,0:T(8,128)}, u32[]{:S(2)}) copy-start(f32[112,128]{1,0:T(8,128)} %get-tuple-element.5) | copy-start | bytes 172036
where the time goes:
time: 39.2 us; the launch traced here: 39 us
  Pallas kernels  34.9 us (89%)
  local copies, waits for them, and re-layouts  3.49 us (9%)
  between operations  0.65 us (2%)
    pallas_call x1, Pallas kernels, per_device(): pl.pallas_call(functools.partial(kernel, n, slots, ring_slots, cols), out...  34.9 us
    unnamed x4, local copies, waits for them, and re-layouts  3.49 us

commit v1 on v0

--- a/solution.py
+++ b/solution.py
@@ -10,6 +10,7 @@
 FFW = 14336
 MESH = pl.DeviceIdType.MESH
 VMEM_ROOM = 67043328
+VMEM_ASK = 24 * 1024 * 1024
 
 
 def ring_place(chip, chips):
@@ -24,10 +25,10 @@
 
 def kernel(
     n, slots, ring_slots, cols,
-    counts_ref, rows_ref, cols_ref, cols_v, tok_hbm, blocks_hbm, up_hbm, rms_ref,
-    tok_ref, blocks_ref, prev_v, last_v, prev_ref, last_ref, held, tok_s, up_ref, sums, sq_s, red_s, res_s,
+    counts_ref, rows_ref, cols_ref, cols_v, tok_hbm, blocks_hbm, up_ref, rms_ref,
+    tok_ref, blocks_ref, prev_v, last_v, prev_ref, last_ref, held, tok_s, sums, sq_s, red_s, res_s,
     ring_send, ring_recv, x_send, x_recv, pd_send, pd_recv,
-    own_send, own_recv, end_send, end_recv, a_send, a_recv, b_send, b_recv, in_sem, up_sem,
+    own_send, own_recv, end_send, end_recv, a_send, a_recv, b_send, b_recv, in_sem,
 ):
     chips = n // 2
     half = chips // 2
@@ -273,13 +274,6 @@
                 device_id_type=MESH,
             )
             scatter[before].start()
-        span = pl.ds(pl.multiple_of(o * wide, wide), wide)
-        up_out.append(
-            pltpu.make_async_copy(up_ref.at[:, span], up_hbm.at[:, span], up_sem.at[e])
-        )
-        if at > 0:
-            up_out[at - 1].start()
-    up_out[-1].start()
     total = sq_s[me]
     for e in range(1, n):
         scatter[e].wait_recv()
@@ -312,8 +306,6 @@
         ).wait_recv()
     for copy in spread:
         copy.wait_send()
-    for copy in up_out:
-        copy.wait()
     for o in range(n):
         rms_ref[o * share : (o + 1) * share, :] = res_s[o]
 
@@ -338,7 +330,7 @@
             jax.ShapeDtypeStruct((cols, edge), jnp.float32),
         ),
         in_specs=[smem, smem, smem, vmem, hbm, hbm],
-        out_specs=(hbm, vmem),
+        out_specs=(vmem, vmem),
         scratch_shapes=[
             pltpu.VMEM(tokens.shape, jnp.bfloat16),
             pltpu.VMEM(blocks.shape, jnp.bfloat16),
@@ -348,7 +340,6 @@
             pltpu.SMEM((1, cols), jnp.int32),
             pltpu.VMEM((n, slots, edge, edge), jnp.bfloat16),
             pltpu.VMEM((width // edge, toks, edge), jnp.bfloat16),
-            pltpu.VMEM((toks, FFW), jnp.bfloat16),
             pltpu.VMEM((n * slots + 1, toks, edge), jnp.float32),
             pltpu.VMEM((n, share, edge), jnp.float32),
             pltpu.VMEM((n, share, edge), jnp.float32),
@@ -368,12 +359,11 @@
             dma((n,)),
             dma((n,)),
             dma((4,)),
-            dma((n,)),
         ],
         compiler_params=pltpu.CompilerParams(
-            collective_id=0, has_side_effects=True, vmem_limit_bytes=VMEM_ROOM
+            collective_id=0, has_side_effects=True, vmem_limit_bytes=VMEM_ASK
         ),
-    )(counts, rows, places, places, tokens, blocks)
+    )(*[pltpu.with_memory_space_constraint(v, pltpu.HBM) for v in (counts, rows, places, places, tokens, blocks)])
     return up, rms.reshape(-1)
 
 

time: 39.2 us -> 36.8 us (0.939)
  local copies, waits for them, and re-layouts: 3.49 us -> 1.86 us
  Pallas kernels: 34.9 us -> 34.1 us
    unnamed x4 -> x2, local copies, waits for them, and re-layouts: 3.49 us -> 1.86 us
    pallas_call x1, Pallas kernels: 34.9 us -> 34.1 us  [per_device(): pl.pallas_call(functools.partial(kernel, n, slots, ring_slots, cols), out...]
where the time goes in v1:
time: 36.8 us; the launch traced here: 36.6 us
  Pallas kernels  34.1 us (93%)
  local copies, waits for them, and re-layouts  1.86 us (5%)
  between operations  0.64 us (2%)
    pallas_call x1, Pallas kernels, per_device(): pl.pallas_call(functools.partial(kernel, n, slots, ring_slots, cols), out...  34.1 us
    unnamed x2, local copies, waits for them, and re-layouts  1.86 us

profile of v1, /device:TPU:0, one launch (start us, length us, event | category | flops | bytes accessed | tf_op | source)
XLA Modules:
  0.0 36.6 jit_solution(14356159701535385825)
XLA Ops:
  0.6 34.1 %shard_map.68 = (bf16[64,14336]{1,0:T(8,128)(2,1)S(1)}, f32[112,128]{1,0:T(8,128)S(1)}) custom-call(s32[2,8]{1,0:T(2,128)} %counts_ref.1, s32[7,16]{1,0:T(8,128)} %bitcast.6, s32[7,16]{1,0:T(8,128)} %bitcast.4, s32[7,16]{1,0:T(8,128)} %bitcast.5, bf16[64,4096]{1,0:T(8,128)(2,1)} %tok_hbm.1, bf16[1,7,128,128]{3,2,1,0:T(8,128)(2,1)} %blocks_hbm.1), custom_call_target="tpu_custom_call" | custom-call | tf_op jit(solution)/shard_map/pallas_call | solution.py:326
  34.7 1.2 %copy.9 = bf16[64,14336]{1,0:T(8,128)(2,1)} copy(bf16[64,14336]{1,0:T(8,128)(2,1)S(1)} %get-tuple-element.8) | data formatting | bytes 3670016
  36.0 0.6 %copy.10 = f32[14336]{0:T(1024)} copy(f32[14336]{0:T(1024)S(1)} %bitcast.3) | data formatting | bytes 114688
